TPU v7x, 32 devices: a whole 2x2x4 slice. The times are simulated.
32 devices in a mesh: bank: 4 (over z), zero: 8 (over y, x, core).
Axes of the slice: x: 2, y: 2, z: 4, core: 2. Of those that a mesh axis runs over, the one named last changes fastest.
Arguments:
- w_gate: float32 [128, 2048, 768], P('bank', 'zero'), may hold values from -0.1875 to 0.1875
- w_up: float32 [128, 2048, 768], P('bank', 'zero'), may hold values from -0.1875 to 0.1875
- router_weight: float32 [2048, 128], P('zero', 'bank'), may hold values from -0.125 to 0.125
- router_gain: float32 [2048], P('zero'), may hold values from 0.25 to 1.75
Outputs:
- serve_gate: bfloat16 [128, 2048, 768], P('bank', None, 'zero')
- serve_up: bfloat16 [128, 2048, 768], P('bank', None, 'zero')
- scale_gate: float32 [128, 768], P('bank', 'zero')
- scale_up: float32 [128, 768], P('bank', 'zero')
- serve_router: bfloat16 [2048, 128], replicated
All inputs are finite; a program needn't handle non-finite values.
Results may differ from a plain program's by a relative error of at most 0.001.
Values may be sent and summed in bfloat16 or wider, within the bound.
A program may use at most 192 MiB of HBM per device.

v0:
```python
import functools

import jax
import jax.numpy as jnp
from jax import lax
from jax.experimental import pallas as pl
from jax.experimental.pallas import tpu as pltpu
from jax.sharding import PartitionSpec as P


def prepare_kernel(parts, w_ref, scale_ref, *refs):
    out_ref = refs[-1]
    normal = w_ref[0] / scale_ref[0]
    turned = normal.T
    width = turned.shape[0] // parts
    for part in range(parts):
        out_ref[part, 0] = turned[part * width : (part + 1) * width].astype(jnp.bfloat16)


def prepare(w, scale, parts, first, count, after):
    _, rows, columns = w.shape
    width = columns // parts
    return pl.pallas_call(
        functools.partial(prepare_kernel, parts),
        grid=(count,),
        in_specs=[
            pl.BlockSpec((1, rows, columns), lambda e: (e + first, 0, 0)),
            pl.BlockSpec((1, 1, columns), lambda e: (e + first, 0, 0)),
        ]
        + [pl.BlockSpec(memory_space=pl.ANY)] * len(after),
        out_specs=pl.BlockSpec((parts, 1, width, rows), lambda e: (0, e, 0, 0)),
        out_shape=jax.ShapeDtypeStruct((parts, count, width, rows), jnp.bfloat16),
        cost_estimate=pl.CostEstimate(
            flops=count * rows * columns * 40,
            bytes_accessed=count * rows * columns * 6,
            transcendentals=0,
        ),
        compiler_params=pltpu.CompilerParams(vmem_limit_bytes=56 * 2**20),
        name="prepare",
    )(w, scale[:, None, :], *after)


def merge_kernel(parts, block_ref, *refs):
    out_ref, token_ref = refs[-2:]
    token_ref[...] = jnp.zeros_like(token_ref)
    rows = block_ref.shape[3]
    for part in range(parts):
        out_ref[0, :, part * rows : (part + 1) * rows] = block_ref[part, 0]


def merge(blocks, before, experts, first):
    parts, count, width, rows = blocks.shape
    chained = before is not None
    return pl.pallas_call(
        functools.partial(merge_kernel, parts),
        grid=(count,),
        in_specs=[pl.BlockSpec((parts, 1, width, rows), lambda e: (0, e, 0, 0))]
        + [pl.BlockSpec(memory_space=pl.ANY)] * chained,
        out_specs=[
            pl.BlockSpec((1, width, parts * rows), lambda e: (e + first, 0, 0)),
            pl.BlockSpec((8, 128), lambda e: (0, 0)),
        ],
        out_shape=[
            jax.ShapeDtypeStruct((experts, width, parts * rows), jnp.bfloat16),
            jax.ShapeDtypeStruct((8, 128), jnp.float32),
        ],
        input_output_aliases={1: 0} if chained else {},
        cost_estimate=pl.CostEstimate(
            flops=count * rows * width * parts * 10,
            bytes_accessed=count * rows * width * parts * 4,
            transcendentals=0,
        ),
        compiler_params=pltpu.CompilerParams(vmem_limit_bytes=56 * 2**20),
        name="merge",
    )(blocks, *([before] if chained else []))


def cuts(experts, small_first):
    small = max(experts * 3 // 16, 1)
    sizes = [small, experts - small] if small_first else [experts - small, small]
    return [size for size in sizes if size]


def shards_blocked(parts, w_gate, w_up, router_weight, router_gain):
    experts, rows, columns = w_gate.shape
    width = columns // parts
    sums = jnp.stack(
        [jnp.sum(w_gate * w_gate, axis=1), jnp.sum(w_up * w_up, axis=1)]
    ).reshape(2 * experts, parts, width)
    pieces = lax.all_to_all(
        sums.transpose(1, 0, 2), "zero", split_axis=0, concat_axis=0, tiled=True
    )
    own = jnp.sqrt(jnp.sum(pieces, axis=0))
    scale_gate, scale_up = own[:experts], own[experts:]

    part_router = (router_weight * router_gain[:, None]).astype(jnp.bfloat16)
    packed = jnp.concatenate(
        [own.reshape(-1), part_router.astype(jnp.float32).reshape(-1)]
    ).reshape(1, -1, 128)
    gathered = lax.all_gather(packed, "zero", axis=0, tiled=True).reshape(parts, -1)
    scales = gathered[:, : own.size].reshape(parts, 2 * experts, width)
    scales = scales.transpose(1, 0, 2).reshape(2 * experts, columns)
    row_router = gathered[:, own.size :].reshape(parts * rows, -1).astype(jnp.bfloat16)

    chunks = [(0, count) for count in cuts(experts, True)]
    chunks += [(1, count) for count in cuts(experts, False)]
    weights, scaled = (w_gate, w_up), (scales[:experts], scales[experts:])
    first, results, tokens, serve_router = [0, 0], [None, None], [], None
    for step, (which, count) in enumerate(chunks):
        after = tokens[step - 2 : step - 1] if step >= 2 else []
        if step == len(chunks) - 1:
            row_router, *after = lax.optimization_barrier((row_router, *after))
            serve_router = lax.all_gather(row_router, "bank", axis=1, tiled=True)
            after = [*after, serve_router]
        pieces = prepare(weights[which], scaled[which], parts, first[which], count, after)
        blocks = lax.all_to_all(pieces, "zero", split_axis=0, concat_axis=0, tiled=True)
        results[which], token = merge(blocks, results[which], experts, first[which])
        tokens.append(token)
        first[which] += count
    return (
        *(result.transpose(0, 2, 1) for result in results),
        scale_gate,
        scale_up,
        serve_router,
    )


def shards_plain(w_gate, w_up, router_weight, router_gain):
    total_gate, total_up = lax.psum(
        (jnp.sum(w_gate * w_gate, axis=1), jnp.sum(w_up * w_up, axis=1)), "zero"
    )
    results, own = [], []
    for w, total in ((w_gate, total_gate), (w_up, total_up)):
        scale = jnp.sqrt(total)
        narrow = (w / jnp.expand_dims(scale, 1)).astype(jnp.bfloat16)
        serve = lax.all_to_all(narrow, "zero", split_axis=2, concat_axis=1, tiled=True)
        width = serve.shape[2]
        results.append(serve)
        own.append(
            lax.dynamic_slice_in_dim(scale, lax.axis_index("zero") * width, width, axis=1)
        )
    part_router = (router_weight * router_gain[:, None]).astype(jnp.bfloat16)
    row_router = lax.all_gather(part_router, "zero", axis=0, tiled=True)
    serve_router = lax.all_gather(row_router, "bank", axis=1, tiled=True)
    return (*results, *own, serve_router)


def solution(mesh):
    parts, banks = mesh.shape["zero"], mesh.shape["bank"]
    placed = (P("bank", "zero", None), P("bank", "zero", None), P("zero", "bank"), P("zero"))

    def shards(w_gate, w_up, router_weight, router_gain):
        experts, rows, columns = w_gate.shape
        width = columns // parts
        packed = 2 * experts * width + router_weight.size
        if rows % 128 == 0 and width % 16 == 0 and packed % 128 == 0:
            return shards_blocked(parts, w_gate, w_up, router_weight, router_gain)
        return shards_plain(w_gate, w_up, router_weight, router_gain)

    return jax.shard_map(
        shards,
        mesh=mesh,
        in_specs=placed,
        out_specs=(
            P("bank", None, "zero"),
            P("bank", None, "zero"),
            P("bank", "zero"),
            P("bank", "zero"),
            P(),
        ),
        check_vma=False,
    )
```

profile of v0, /device:TPU:0, one launch (start us, length us, event | category | flops | bytes accessed | tf_op | source)
XLA Modules:
  0.0 357.1 jit_solution(18070718905446957507)
XLA Ops:
  0.6 9.5 %multiply_reduce_fusion.1 = f32[32,768]{1,0:T(8,128)S(1)} fusion(f32[32,256,768]{2,1,0:T(8,128)} %w_ref.5), kind=kLoop, calls=%fused_computation.1 | loop fusion | flops 12558336 | bytes 25264128 | tf_op jit(solution)/shard_map/reduce_sum | solution.py:88
  10.1 6.0 %copy-done = f32[32,256,768]{2,1,0:T(8,128)S(1)} copy-done((f32[32,256,768]{2,1,0:T(8,128)S(1)}, f32[32,256,768]{2,1,0:T(8,128)}, u32[]{:S(2)}) %copy-start) | copy-done | bytes 25165848
  16.1 1.9 multiply_reduce_fusion
  18.2 0.8 copy.20
  19.0 5.2 %all-to-all-start = ((f32[8,64,96]{2,1,0:T(8,128)}), f32[8,64,96]{2,1,0:T(8,128)S(1)}, u32[]{:S(2)}, u32[]{:S(2)}) async-start(f32[8,64,96]{2,1,0:T(8,128)} %copy.20), calls=%async_computation | async-start | bytes 524288 | tf_op jit(solution)/shard_map/all_to_all | solution.py:90
  24.4 6.7 %all-to-all-done = f32[8,64,96]{2,1,0:T(8,128)S(1)} async-done(((f32[8,64,96]{2,1,0:T(8,128)}), f32[8,64,96]{2,1,0:T(8,128)S(1)}, u32[]{:S(2)}, u32[]{:S(2)}) %all-to-all-start) | async-done | bytes 196640 | tf_op jit(solution)/shard_map/all_to_all | solution.py:90
  31.2 8.8 %all_gather.6 = f32[8,112,128]{2,1,0:T(8,128)S(1)} all-gather(f32[1,112,128]{2,1,0:T(8,128)S(1)} %maximum_bitcast_fusion), channel_id=1, replica_groups=mesh['bank'=4,'zero'=8] {'zero'}, dimensions={0}, use_global_device_ids=true | all-gather | bytes 516096 | tf_op jit(solution)/shard_map/all_gather | solution.py:100
  40.0 0.1 copy.29
  40.4 0.8 broadcast_in_dim.4.scale_ref
  41.2 5.8 %prepare.5 = bf16[8,6,96,256]{3,2,1,0:T(8,128)(2,1)} custom-call(f32[32,256,768]{2,1,0:T(8,128)} %w_ref.5, f32[32,1,768]{2,1,0:T(1,128)} %broadcast_in_dim.4.scale_ref), custom_call_target="tpu_custom_call" | custom-call | flops 47185920 | bytes 7077888 | tf_op jit(solution)/shard_map/prepare/pallas_call | solution.py:23
  47.0 3.6 %all-to-all-start.2 = ((bf16[8,6,96,256]{3,2,1,0:T(8,128)(2,1)}), bf16[8,6,96,256]{3,2,1,0:T(8,128)(2,1)S(1)}, u32[]{:S(2)}, u32[]{:S(2)}) async-start(bf16[8,6,96,256]{3,2,1,0:T(8,128)(2,1)} %prepare.5), calls=%async_computation.2 | async-start | bytes 4718592 | tf_op jit(solution)/shard_map/all_to_all | solution.py:116
  50.7 21.1 %prepare.4 = bf16[8,26,96,256]{3,2,1,0:T(8,128)(2,1)} custom-call(f32[32,256,768]{2,1,0:T(8,128)} %w_ref.5, f32[32,1,768]{2,1,0:T(1,128)} %broadcast_in_dim.4.scale_ref), custom_call_target="tpu_custom_call" | custom-call | flops 204472320 | bytes 30670848 | tf_op jit(solution)/shard_map/prepare/pallas_call | solution.py:23
  71.8 8.2 %all-to-all-done.2.block_ref = bf16[8,6,96,256]{3,2,1,0:T(8,128)(2,1)S(1)} async-done(((bf16[8,6,96,256]{3,2,1,0:T(8,128)(2,1)}), bf16[8,6,96,256]{3,2,1,0:T(8,128)(2,1)S(1)}, u32[]{:S(2)}, u32[]{:S(2)}) %all-to-all-start.2) | async-done | bytes 2359328 | tf_op jit(solution)/shard_map/all_to_all | solution.py:116
  80.0 5.1 %all-to-all-start.1 = ((bf16[8,26,96,256]{3,2,1,0:T(8,128)(2,1)}), bf16[8,26,96,256]{3,2,1,0:T(8,128)(2,1)}, u32[]{:S(2)}, u32[]{:S(2)}) async-start(bf16[8,26,96,256]{3,2,1,0:T(8,128)(2,1)} %prepare.4), calls=%async_computation.1 | async-start | bytes 20447232 | tf_op jit(solution)/shard_map/all_to_all | solution.py:116
  85.2 0.8 broadcast_in_dim.10.scale_ref
  86.1 4.9 %merge.4 = (bf16[32,96,2048]{2,1,0:T(8,128)(2,1)}, f32[8,128]{1,0:T(8,128)}) custom-call(bf16[8,6,96,256]{3,2,1,0:T(8,128)(2,1)} %copy-done.2), custom_call_target="tpu_custom_call" | custom-call | flops 11796480 | bytes 4718592 | tf_op jit(solution)/shard_map/merge/pallas_call | solution.py:54
  91.0 21.1 %prepare.7 = bf16[8,26,96,256]{3,2,1,0:T(8,128)(2,1)} custom-call(f32[32,256,768]{2,1,0:T(8,128)} %w_ref.7, f32[32,1,768]{2,1,0:T(1,128)} %broadcast_in_dim.10.scale_ref, f32[8,128]{1,0:T(8,128)} %get-tuple-element.18.refs_0_), custom_call_target="tpu_custom_call" | custom-call | flops 204472320 | bytes 30670848 | tf_op jit(solution)/shard_map/prepare/pallas_call | solution.py:23
  112.1 86.8 %all-to-all-done.1.block_ref = bf16[8,26,96,256]{3,2,1,0:T(8,128)(2,1)} async-done(((bf16[8,26,96,256]{3,2,1,0:T(8,128)(2,1)}), bf16[8,26,96,256]{3,2,1,0:T(8,128)(2,1)}, u32[]{:S(2)}, u32[]{:S(2)}) %all-to-all-start.1) | async-done | bytes 10223648 | tf_op jit(solution)/shard_map/all_to_all | solution.py:116
  198.9 5.2 %all-to-all-start.4 = ((bf16[8,26,96,256]{3,2,1,0:T(8,128)(2,1)}), bf16[8,26,96,256]{3,2,1,0:T(8,128)(2,1)}, u32[]{:S(2)}, u32[]{:S(2)}) async-start(bf16[8,26,96,256]{3,2,1,0:T(8,128)(2,1)} %prepare.7), calls=%async_computation.4 | async-start | bytes 20447232 | tf_op jit(solution)/shard_map/all_to_all | solution.py:116
  204.0 0.4 convert_element_type.9
  204.4 17.1 %merge.5 = (bf16[32,96,2048]{2,1,0:T(8,128)(2,1)}, f32[8,128]{1,0:T(8,128)}) custom-call(bf16[8,26,96,256]{3,2,1,0:T(8,128)(2,1)} %all-to-all-done.1.block_ref, bf16[32,96,2048]{2,1,0:T(8,128)(2,1)} %get-tuple-element.13.refs_0_), custom_call_target="tpu_custom_call", output_to_operand_aliasing={{0}: (1, {})} | custom-call | flops 51118080 | bytes 20447232 | tf_op jit(solution)/shard_map/merge/pallas_call | solution.py:54
  221.5 0.2 copy.24
  221.7 16.3 %all_gather.7 = bf16[2048,128]{0,1:T(8,128)(2,1)S(1)} all-gather(bf16[2048,32]{0,1:T(8,128)(2,1)S(1)} %copy.24), channel_id=1, replica_groups=mesh['bank'=4,'zero'=8] {'bank'}, dimensions={1}, use_global_device_ids=true | all-gather | bytes 655360 | tf_op jit(solution)/shard_map/all_gather | solution.py:113
  238.0 1.0 copy.25.refs_1_
  239.0 5.8 %prepare.6 = bf16[8,6,96,256]{3,2,1,0:T(8,128)(2,1)} custom-call(f32[32,256,768]{2,1,0:T(8,128)} %w_ref.7, f32[32,1,768]{2,1,0:T(1,128)} %broadcast_in_dim.10.scale_ref, f32[8,128]{1,0:T(8,128)} %get-tuple-element.16.refs_0_, bf16[2048,128]{1,0:T(8,128)(2,1)} %copy.25.refs_1_), custom_call_target="tpu_custom_call" | custom-call | flops 47185920 | bytes 7077888 | tf_op jit(solution)/shard_map/prepare/pallas_call | solution.py:23
  244.8 72.9 %all-to-all-done.4.block_ref = bf16[8,26,96,256]{3,2,1,0:T(8,128)(2,1)} async-done(((bf16[8,26,96,256]{3,2,1,0:T(8,128)(2,1)}), bf16[8,26,96,256]{3,2,1,0:T(8,128)(2,1)}, u32[]{:S(2)}, u32[]{:S(2)}) %all-to-all-start.4) | async-done | bytes 10223648 | tf_op jit(solution)/shard_map/all_to_all | solution.py:116
  317.7 3.6 %all-to-all-start.3 = ((bf16[8,6,96,256]{3,2,1,0:T(8,128)(2,1)}), bf16[8,6,96,256]{3,2,1,0:T(8,128)(2,1)S(1)}, u32[]{:S(2)}, u32[]{:S(2)}) async-start(bf16[8,6,96,256]{3,2,1,0:T(8,128)(2,1)} %prepare.6), calls=%async_computation.3 | async-start | bytes 4718592 | tf_op jit(solution)/shard_map/all_to_all | solution.py:116
  321.3 0.6 fusion.2
  322.0 17.1 %merge.6 = (bf16[32,96,2048]{2,1,0:T(8,128)(2,1)}, f32[8,128]{1,0:T(8,128)}) custom-call(bf16[8,26,96,256]{3,2,1,0:T(8,128)(2,1)} %all-to-all-done.4.block_ref), custom_call_target="tpu_custom_call" | custom-call | flops 51118080 | bytes 20447232 | tf_op jit(solution)/shard_map/merge/pallas_call | solution.py:54
  339.0 11.7 %all-to-all-done.3.block_ref = bf16[8,6,96,256]{3,2,1,0:T(8,128)(2,1)S(1)} async-done(((bf16[8,6,96,256]{3,2,1,0:T(8,128)(2,1)}), bf16[8,6,96,256]{3,2,1,0:T(8,128)(2,1)S(1)}, u32[]{:S(2)}, u32[]{:S(2)}) %all-to-all-start.3) | async-done | bytes 2359328 | tf_op jit(solution)/shard_map/all_to_all | solution.py:116
  350.7 1.4 copy-done.1
  352.1 4.9 %merge.7 = (bf16[32,96,2048]{2,1,0:T(8,128)(2,1)}, f32[8,128]{1,0:T(8,128)}) custom-call(bf16[8,6,96,256]{3,2,1,0:T(8,128)(2,1)} %copy-done.1, bf16[32,96,2048]{2,1,0:T(8,128)(2,1)} %get-tuple-element.19.refs_0_), custom_call_target="tpu_custom_call", output_to_operand_aliasing={{0}: (1, {})} | custom-call | flops 11796480 | bytes 4718592 | tf_op jit(solution)/shard_map/merge/pallas_call | solution.py:54
  (23 shorter events, 0.8 us)
Async XLA Ops:
  0.6 15.5 %copy-start = (f32[32,256,768]{2,1,0:T(8,128)S(1)}, f32[32,256,768]{2,1,0:T(8,128)}, u32[]{:S(2)}) copy-start(f32[32,256,768]{2,1,0:T(8,128)} %w_ref.7) | copy-start | bytes 75497472
  16.1 8.1 %copy-start.3 = (f32[256,32]{0,1:T(8,128)S(1)}, f32[256,32]{0,1:T(8,128)}, u32[]{:S(2)}) copy-start(f32[256,32]{0,1:T(8,128)} %param.6) | copy-start | bytes 98308
  16.1 8.1 %copy-start.4 = (f32[256]{0:T(256)S(1)}, f32[256]{0:T(256)}, u32[]{:S(2)}) copy-start(f32[256]{0:T(256)} %param.7) | copy-start | bytes 3076
  19.0 12.1 %all-to-all-start = ((f32[8,64,96]{2,1,0:T(8,128)}), f32[8,64,96]{2,1,0:T(8,128)S(1)}, u32[]{:S(2)}, u32[]{:S(2)}) async-start(f32[8,64,96]{2,1,0:T(8,128)} %copy.20), calls=%async_computation | async-start | bytes 524288 | tf_op jit(solution)/shard_map/all_to_all | solution.py:90
  47.0 33.0 %all-to-all-start.2 = ((bf16[8,6,96,256]{3,2,1,0:T(8,128)(2,1)}), bf16[8,6,96,256]{3,2,1,0:T(8,128)(2,1)S(1)}, u32[]{:S(2)}, u32[]{:S(2)}) async-start(bf16[8,6,96,256]{3,2,1,0:T(8,128)(2,1)} %prepare.5), calls=%async_computation.2 | async-start | bytes 4718592 | tf_op jit(solution)/shard_map/all_to_all | solution.py:116
  80.0 6.0 %copy-start.2 = (bf16[8,6,96,256]{3,2,1,0:T(8,128)(2,1)}, bf16[8,6,96,256]{3,2,1,0:T(8,128)(2,1)S(1)}, u32[]{:S(2)}) copy-start(bf16[8,6,96,256]{3,2,1,0:T(8,128)(2,1)S(1)} %all-to-all-done.2.block_ref) | copy-start | bytes 7077892
  80.0 118.8 %all-to-all-start.1 = ((bf16[8,26,96,256]{3,2,1,0:T(8,128)(2,1)}), bf16[8,26,96,256]{3,2,1,0:T(8,128)(2,1)}, u32[]{:S(2)}, u32[]{:S(2)}) async-start(bf16[8,26,96,256]{3,2,1,0:T(8,128)(2,1)} %prepare.4), calls=%async_computation.1 | async-start | bytes 20447232 | tf_op jit(solution)/shard_map/all_to_all | solution.py:116
  198.9 118.9 %all-to-all-start.4 = ((bf16[8,26,96,256]{3,2,1,0:T(8,128)(2,1)}), bf16[8,26,96,256]{3,2,1,0:T(8,128)(2,1)}, u32[]{:S(2)}, u32[]{:S(2)}) async-start(bf16[8,26,96,256]{3,2,1,0:T(8,128)(2,1)} %prepare.7), calls=%async_computation.4 | async-start | bytes 20447232 | tf_op jit(solution)/shard_map/all_to_all | solution.py:116
  317.7 33.0 %all-to-all-start.3 = ((bf16[8,6,96,256]{3,2,1,0:T(8,128)(2,1)}), bf16[8,6,96,256]{3,2,1,0:T(8,128)(2,1)S(1)}, u32[]{:S(2)}, u32[]{:S(2)}) async-start(bf16[8,6,96,256]{3,2,1,0:T(8,128)(2,1)} %prepare.6), calls=%async_computation.3 | async-start | bytes 4718592 | tf_op jit(solution)/shard_map/all_to_all | solution.py:116
  350.7 1.4 copy-start.1
where the time goes:
time: 360 us; the launch traced here: 357 us
  waiting for transfers between devices  186 us (52%)
  Pallas kernels  97.9 us (27%)
  blocking collectives  25.1 us (7%)
  starting transfers between devices  22.7 us (6%)
  local copies, waits for them, and re-layouts  12.9 us (4%)
  other arithmetic  11.5 us (3%)
    all_to_all x4, waiting for transfers between devices, shards_blocked(): lax.all_to_all(pieces, 'zero', split_axis=0, concat_axis=0, tiled=True)  180 us
    pallas_call x4, Pallas kernels, prepare(): pl.pallas_call(functools.partial(prepare_kernel, parts), grid=(count,), i...  53.9 us
    pallas_call x4, Pallas kernels, merge(): pl.pallas_call(functools.partial(merge_kernel, parts), grid=(count,), in_...  44 us
    all_to_all x4, starting transfers between devices, shards_blocked(): lax.all_to_all(pieces, 'zero', split_axis=0, concat_axis=0, tiled=True)  17.5 us
    all_gather x1, blocking collectives, shards_blocked(): serve_router = lax.all_gather(row_router, 'bank', axis=1, tiled=True)  16.3 us
    reduce_sum x1, other arithmetic, shards_blocked(): jnp.sum(w_gate * w_gate, axis=1)  9.5 us
    all_gather x1, blocking collectives, shards_blocked(): lax.all_gather(packed, 'zero', axis=0, tiled=True).reshape(parts, -1)  8.77 us
    unnamed x11, local copies, waits for them, and re-layouts  7.56 us
  transfers between devices with their start and end apart: 5, of which 5 were waited for; matrix products, arithmetic and copies ran while one was open for 1% of the time, Pallas kernels for 24%

commit v1 on v0

v1 whole, which is shorter than its diff:
```python
import functools

import jax
import jax.numpy as jnp
from jax import lax
from jax.experimental import pallas as pl
from jax.experimental.pallas import tpu as pltpu
from jax.sharding import PartitionSpec as P

MESH = pl.DeviceIdType.MESH
AHEAD = 2
VMEM_LIMIT = 32 * 2**20
SLOTS = 8


def flip(index, mask, bits):
    out = 0
    for bit in range(bits):
        here = lax.rem(lax.div(index, 2**bit), 2)
        out = out + (1 - here if (mask >> bit) & 1 else here) * 2**bit
    return out


def exchange_kernel(
    parts,
    banks,
    gate_ref,
    up_ref,
    router_ref,
    gain_ref,
    landing,
    scale_out,
    router_out,
    ring,
    outgoing,
    sums,
    sums_in,
    scales,
    row_router,
    routers,
    load_sem,
    send_sem,
    recv_sem,
    sum_send,
    sum_recv,
    scale_send,
    scale_recv,
    row_send,
    row_recv,
    bank_send,
    bank_recv,
):
    experts, rows, columns = gate_ref.shape
    width = columns // parts
    total = 2 * experts
    batches = total // parts
    depth = ring.shape[0]
    bits = parts.bit_length() - 1
    me, bank = lax.axis_index("zero"), lax.axis_index("bank")
    masks = sorted(range(1, parts), key=lambda m: (m == 1, m % 2, -(m // 2)))
    peers = [flip(me, mask, bits) for mask in masks]
    own_rows = pl.ds(pl.multiple_of(me * rows, 128), rows)

    def remote(src, dst, send, recv, **device):
        return pltpu.make_async_remote_copy(
            src_ref=src,
            dst_ref=dst,
            send_sem=send,
            recv_sem=recv,
            device_id=device,
            device_id_type=MESH,
        )

    def load(e):
        slot = lax.rem(e, depth)

        @pl.when(e < experts)
        def _():
            pltpu.make_async_copy(gate_ref.at[e], ring.at[slot], load_sem.at[slot]).start()

        @pl.when(e >= experts)
        def _():
            pltpu.make_async_copy(
                up_ref.at[e - experts], ring.at[slot], load_sem.at[slot]
            ).start()

    def square(e):
        slot = lax.rem(e, depth)
        pltpu.make_async_copy(gate_ref.at[0], ring.at[slot], load_sem.at[slot]).wait()
        w = ring[slot]
        sums[e] = jnp.sum(w * w, axis=0, keepdims=True)

    def send_sums(b):
        for peer in peers:
            remote(
                sums.at[b * parts + peer],
                sums_in.at[b, me],
                sum_send.at[b],
                sum_recv.at[b],
                zero=peer,
            ).start()

    def others(ref):
        return ref.at[pl.ds(0, parts - 1)]

    def finish_sums(b):
        remote(
            others(sums_in.at[b]), others(sums_in.at[b]), sum_send.at[b], sum_recv.at[b], zero=me
        ).wait_recv()
        sums_in[b, me] = sums[b * parts + me]
        whole = sums_in[b, 0]
        for part in range(1, parts):
            whole = whole + sums_in[b, part]
        scales[b * parts + me] = jnp.sqrt(whole)
        row = scales.at[b * parts + me]
        for peer in peers:
            remote(row, row, scale_send.at[b], scale_recv.at[b], zero=peer).start()

    def wait_scales(b):
        remote(
            others(scales), others(scales), scale_send.at[b], scale_recv.at[b], zero=me
        ).wait_recv()

    def keep_scales(b):
        first = pl.multiple_of(b * parts, 8)
        whole = jnp.concatenate([scales[b * parts + j] for j in range(parts)], axis=0)
        own = jnp.zeros((parts, width), jnp.float32)
        for part in range(parts):
            own = jnp.where(me == part, whole[:, part * width : (part + 1) * width], own)
        scale_out[pl.ds(first, parts), :] = own

    def send_piece(e, slot, at):
        return remote(
            outgoing.at[slot, peers[at]],
            landing.at[e, :, own_rows],
            send_sem.at[slot, at],
            recv_sem.at[me],
            zero=peers[at],
        )

    def row_piece(peer):
        return remote(
            row_router, routers.at[bank, :, own_rows], row_send, row_recv, zero=peer
        )

    def all_rows():
        part = routers.at[bank, :, pl.ds(0, (parts - 1) * rows)]
        return remote(part, part, row_send, row_recv, zero=me)

    def bank_piece(step):
        other = lax.rem(bank + step, banks)
        return remote(
            routers.at[bank], routers.at[bank], bank_send, bank_recv, bank=other
        )

    def all_banks():
        part = routers.at[pl.ds(0, banks - 1)]
        return remote(part, part, bank_send, bank_recv, zero=me)

    lax.fori_loop(0, depth, lambda e, c: (load(e), c)[1], 0)

    barrier = pltpu.get_barrier_semaphore()
    for peer in peers:
        pl.semaphore_signal(barrier, inc=1, device_id={"zero": peer}, device_id_type=MESH)
    for step in range(1, banks):
        pl.semaphore_signal(
            barrier,
            inc=1,
            device_id={"bank": lax.rem(bank + step, banks)},
            device_id_type=MESH,
        )

    lax.fori_loop(0, parts, lambda e, c: (square(e), c)[1], 0)
    pl.semaphore_wait(barrier, parts - 1 + banks - 1)
    send_sums(0)
    part_router = (router_ref[...] * gain_ref[...]).astype(jnp.bfloat16)
    row_router[...] = part_router
    routers[bank, :, own_rows] = part_router
    lax.fori_loop(parts, AHEAD * parts, lambda e, c: (square(e), c)[1], 0)
    finish_sums(0)
    for b in range(1, AHEAD):
        send_sums(b)

    def step(s, carry):
        b, i = lax.div(s, parts), lax.rem(s, parts)
        slot = lax.rem(s, SLOTS)

        @pl.when(i == 0)
        def _():
            wait_scales(b)

        @pl.when(s >= SLOTS)
        def _():
            for at in range(parts - 1):
                send_piece(s, slot, at).wait_send()

        turned = (ring[lax.rem(s, depth)] / scales[s]).T
        for part in range(parts):
            outgoing[slot, part] = turned[part * width : (part + 1) * width].astype(
                jnp.bfloat16
            )
        landing[s, :, own_rows] = outgoing[slot, me]

        @pl.when(s + depth < total)
        def _():
            load(s + depth)

        for at in range(parts - 1):
            send_piece(s, slot, at).start()

        @pl.when(s + AHEAD * parts < total)
        def _():
            square(s + AHEAD * parts)

        @pl.when(jnp.logical_and(i == parts - 1, b + AHEAD < batches))
        def _():
            send_sums(b + AHEAD)

        @pl.when(jnp.logical_and(i == parts // 2, b + 1 < batches))
        def _():
            finish_sums(b + 1)

        @pl.when(i == 2)
        def _():
            keep_scales(b)

        @pl.when(s == 1)
        def _():
            for peer in peers:
                row_piece(peer).start()

        @pl.when(s == total // 4)
        def _():
            all_rows().wait_recv()
            for hop in range(1, banks):
                bank_piece(hop).start()

        return carry

    lax.fori_loop(0, total, step, 0)

    all_banks().wait_send()
    all_banks().wait_recv()
    all_rows().wait_send()
    turned = routers[...].reshape(banks * router_ref.shape[0], parts * rows).T
    router_out[...] = turned

    for b in range(batches):
        for sems, buffer in ((sum_send, sums_in.at[0]), (scale_send, scales)):
            remote(others(buffer), others(buffer), sems.at[b], sems.at[b], zero=me).wait_send()
    for s in range(total - SLOTS, total):
        for at in range(parts - 1):
            send_piece(s, s % SLOTS, at).wait_send()
    for peer in peers:
        region = landing.at[:, :, pl.ds(pl.multiple_of(peer * rows, 128), rows)]
        remote(region, region, recv_sem.at[me], recv_sem.at[peer], zero=me).wait_recv()


def exchange(parts, banks, w_gate, w_up, router_weight, router_gain):
    experts, rows, columns = w_gate.shape
    width = columns // parts
    total = 2 * experts
    batches = total // parts
    held = router_weight.shape[1]
    vmem = pl.BlockSpec(memory_space=pltpu.VMEM)
    hbm = pl.BlockSpec(memory_space=pl.ANY)
    depth = (AHEAD + 1) * parts
    dma = pltpu.SemaphoreType.DMA
    return pl.pallas_call(
        functools.partial(exchange_kernel, parts, banks),
        in_specs=[hbm, hbm, vmem, vmem],
        out_specs=[vmem] * 3,
        out_shape=[
            pltpu.VMEM((total, width, parts * rows), jnp.bfloat16),
            pltpu.VMEM((total, width), jnp.float32),
            pltpu.VMEM((parts * rows, banks * held), jnp.bfloat16),
        ],
        scratch_shapes=[
            pltpu.VMEM((depth, rows, columns), jnp.float32),
            pltpu.VMEM((SLOTS, parts, width, rows), jnp.bfloat16),
            pltpu.VMEM((total, 1, columns), jnp.float32),
            pltpu.VMEM((batches, parts, 1, columns), jnp.float32),
            pltpu.VMEM((total, 1, columns), jnp.float32),
            pltpu.VMEM((held, rows), jnp.bfloat16),
            pltpu.VMEM((banks, held, parts * rows), jnp.bfloat16),
            dma((depth,)),
            dma((SLOTS, parts - 1)),
            dma((parts,)),
            dma((batches,)),
            dma((batches,)),
            dma((batches,)),
            dma((batches,)),
            dma,
            dma,
            dma,
            dma,
        ],
        cost_estimate=pl.CostEstimate(
            flops=total * rows * columns * 60,
            bytes_accessed=total * rows * columns * 4,
            transcendentals=0,
        ),
        compiler_params=pltpu.CompilerParams(
            collective_id=0, has_side_effects=True, vmem_limit_bytes=VMEM_LIMIT
        ),
        name="exchange",
    )(
        pltpu.with_memory_space_constraint(w_gate, pltpu.HBM),
        pltpu.with_memory_space_constraint(w_up, pltpu.HBM),
        router_weight.T,
        router_gain[None, :],
    )


def deliver_kernel(pieces, landing, scales, router, gate, up, scale_gate, scale_up, out, sem):
    experts = gate.shape[0]
    size = experts // pieces
    copies = []
    for which, target in enumerate((gate, up)):
        for piece in range(pieces):
            copies.append(
                (
                    landing.at[pl.ds(which * experts + piece * size, size)],
                    target.at[pl.ds(piece * size, size)],
                )
            )
    copies.append((scales.at[pl.ds(0, experts)], scale_gate))
    copies.append((scales.at[pl.ds(experts, experts)], scale_up))
    copies.append((router, out))
    handles = [
        pltpu.make_async_copy(source, target, sem.at[at])
        for at, (source, target) in enumerate(copies)
    ]
    for handle in handles:
        handle.start()
    for handle in handles:
        handle.wait()


def deliver(landing, scales, router):
    total, width, rows = landing.shape
    experts = total // 2
    pieces = 8 if experts % 8 == 0 else 1
    vmem = pl.BlockSpec(memory_space=pltpu.VMEM)
    hbm = pl.BlockSpec(memory_space=pl.ANY)
    return pl.pallas_call(
        functools.partial(deliver_kernel, pieces),
        in_specs=[vmem] * 3,
        out_specs=[hbm] * 5,
        out_shape=[
            jax.ShapeDtypeStruct((experts, width, rows), landing.dtype),
            jax.ShapeDtypeStruct((experts, width, rows), landing.dtype),
            jax.ShapeDtypeStruct((experts, width), jnp.float32),
            jax.ShapeDtypeStruct((experts, width), jnp.float32),
            jax.ShapeDtypeStruct(router.shape, router.dtype),
        ],
        scratch_shapes=[pltpu.SemaphoreType.DMA((2 * pieces + 3,))],
        cost_estimate=pl.CostEstimate(
            flops=total * rows * width, bytes_accessed=4 * total * rows * width, transcendentals=0
        ),
        compiler_params=pltpu.CompilerParams(vmem_limit_bytes=2**20),
        name="deliver",
    )(*(pltpu.with_memory_space_constraint(x, pltpu.VMEM) for x in (landing, scales, router)))


def shards_blocked(parts, banks, w_gate, w_up, router_weight, router_gain):
    arrived = exchange(parts, banks, w_gate, w_up, router_weight, router_gain)
    gate, up, scale_gate, scale_up, router = deliver(*arrived)
    return gate.transpose(0, 2, 1), up.transpose(0, 2, 1), scale_gate, scale_up, router


def shards_plain(w_gate, w_up, router_weight, router_gain):
    total_gate, total_up = lax.psum(
        (jnp.sum(w_gate * w_gate, axis=1), jnp.sum(w_up * w_up, axis=1)), "zero"
    )
    results, own = [], []
    for w, total in ((w_gate, total_gate), (w_up, total_up)):
        scale = jnp.sqrt(total)
        narrow = (w / jnp.expand_dims(scale, 1)).astype(jnp.bfloat16)
        serve = lax.all_to_all(narrow, "zero", split_axis=2, concat_axis=1, tiled=True)
        width = serve.shape[2]
        results.append(serve)
        own.append(
            lax.dynamic_slice_in_dim(scale, lax.axis_index("zero") * width, width, axis=1)
        )
    part_router = (router_weight * router_gain[:, None]).astype(jnp.bfloat16)
    row_router = lax.all_gather(part_router, "zero", axis=0, tiled=True)
    serve_router = lax.all_gather(row_router, "bank", axis=1, tiled=True)
    return (*results, *own, serve_router)


def solution(mesh):
    parts, banks = mesh.shape["zero"], mesh.shape["bank"]
    placed = (P("bank", "zero", None), P("bank", "zero", None), P("zero", "bank"), P("zero"))

    def shards(w_gate, w_up, router_weight, router_gain):
        experts, rows, columns = w_gate.shape
        held = router_weight.shape[1]
        total = 2 * experts
        power = parts & (parts - 1) == 0 and parts % 8 == 0
        whole = rows % 128 == 0 and columns % (16 * parts) == 0 and held % 16 == 0
        if power and whole and total % parts == 0 and total >= (AHEAD + 1) * parts:
            return shards_blocked(parts, banks, w_gate, w_up, router_weight, router_gain)
        return shards_plain(w_gate, w_up, router_weight, router_gain)

    return jax.shard_map(
        shards,
        mesh=mesh,
        in_specs=placed,
        out_specs=(
            P("bank", None, "zero"),
            P("bank", None, "zero"),
            P("bank", "zero"),
            P("bank", "zero"),
            P(),
        ),
        check_vma=False,
    )
```

time: 360 us -> 300 us (0.83)
  Pallas kernels: 97.9 us -> 299 us
  waiting for transfers between devices: 186 us -> 0 us
  blocking collectives: 25.1 us -> 0 us
  starting transfers between devices: 22.7 us -> 0 us
  local copies, waits for them, and re-layouts: 12.9 us -> 0 us
  other arithmetic: 11.5 us -> 0 us
    pallas_call x8 -> x2, Pallas kernels: 97.9 us -> 299 us  [the longest x1 290 us: exchange(): pl.pallas_call(functools.partial(exchange_kernel, parts, banks), in_specs...]
    all_to_all x5 -> x0, waiting for transfers between devices: 186 us -> none  [the longest x4 180 us: shards_blocked(): lax.all_to_all(pieces, 'zero', split_axis=0, concat_axis=0, tiled=True)]
    all_gather x2 -> x0, blocking collectives: 25.1 us -> none  [the longest x1 16.3 us: shards_blocked(): serve_router = lax.all_gather(row_router, 'bank', axis=1, tiled=True)]
    all_to_all x5 -> x0, starting transfers between devices: 22.7 us -> none  [the longest x4 17.5 us: shards_blocked(): lax.all_to_all(pieces, 'zero', split_axis=0, concat_axis=0, tiled=True)]
    reduce_sum x3 -> x0, other arithmetic: 11.5 us -> none  [the longest x1 9.5 us: shards_blocked(): jnp.sum(w_gate * w_gate, axis=1)]
    unnamed x11 -> x0, local copies, waits for them, and re-layouts: 7.56 us -> none
  transfers between devices with their start and end apart: 5 -> 0, of which waited for: 5 -> 0; matrix products, arithmetic and copies ran while one was open for 1% -> 0% of each run, Pallas kernels for 24% -> 0%
where the time goes in v1:
time: 300 us; the launch traced here: 299 us
  Pallas kernels  299 us (100%)
    pallas_call x1, Pallas kernels, exchange(): pl.pallas_call(functools.partial(exchange_kernel, parts, banks), in_specs...  290 us
    pallas_call x1, Pallas kernels, deliver(): pl.pallas_call(functools.partial(deliver_kernel, pieces), in_specs=[vmem]...  8.67 us

profile of v1, /device:TPU:0, one launch (start us, length us, event | category | flops | bytes accessed | tf_op | source)
XLA Modules:
  0.0 299.2 jit_solution(11407570004138619761)
XLA Ops:
  0.6 289.9 %exchange.1 = (bf16[64,96,2048]{2,1,0:T(8,128)(2,1)S(1)}, f32[64,96]{1,0:T(8,128)S(1)}, bf16[2048,128]{1,0:T(8,128)(2,1)S(1)}) custom-call(f32[32,256,768]{2,1,0:T(8,128)} %gate_ref.1, f32[32,256,768]{2,1,0:T(8,128)} %up_ref.1, f32[32,256]{1,0:T(8,128)} %bitcast.4, f32[1,256]{1,0:T(1,128)} %bitcast.5), custom_call_target="tpu_custom_call" | custom-call | flops 754974720 | bytes 50331648 | tf_op jit(solution)/shard_map/exchange/pallas_call | solution.py:269
  290.6 8.7 %deliver.1 = (bf16[32,96,2048]{2,1,0:T(8,128)(2,1)}, bf16[32,96,2048]{2,1,0:T(8,128)(2,1)}, f32[32,96]{1,0:T(8,128)}, f32[32,96]{1,0:T(8,128)}, bf16[2048,128]{1,0:T(8,128)(2,1)}) custom-call(bf16[64,96,2048]{2,1,0:T(8,128)(2,1)S(1)} %get-tuple-element.13.landing, f32[64,96]{1,0:T(8,128)S(1)} %get-tuple-element.14.scales, ...), custom_call_target="tpu_custom_call" | custom-call | flops 12582912 | bytes 50331648 | tf_op jit(solution)/shard_map/deliver/pallas_call | solution.py:346

commit v2 on v1

--- a/solution.py
+++ b/solution.py
@@ -8,7 +8,8 @@
 from jax.sharding import PartitionSpec as P
 
 MESH = pl.DeviceIdType.MESH
-AHEAD = 2
+FIRST = 2
+LOADS = 4
 VMEM_LIMIT = 32 * 2**20
 SLOTS = 8
 
@@ -33,18 +34,21 @@
     router_out,
     ring,
     outgoing,
+    first_in,
     sums,
-    sums_in,
+    pair_in,
+    chip_sums,
+    chip_in,
     scales,
     row_router,
     routers,
     load_sem,
     send_sem,
     recv_sem,
-    sum_send,
-    sum_recv,
-    scale_send,
-    scale_recv,
+    first_send,
+    first_recv,
+    batch_send,
+    batch_recv,
     row_send,
     row_recv,
     bank_send,
@@ -54,11 +58,15 @@
     width = columns // parts
     total = 2 * experts
     batches = total // parts
+    half = parts // 2
     depth = ring.shape[0]
     bits = parts.bit_length() - 1
     me, bank = lax.axis_index("zero"), lax.axis_index("bank")
+    side, place = lax.rem(me, 2), lax.div(me, 2)
     masks = sorted(range(1, parts), key=lambda m: (m == 1, m % 2, -(m // 2)))
     peers = [flip(me, mask, bits) for mask in masks]
+    partner = flip(me, 1, bits)
+    cohort = [flip(me, mask, bits) for mask in masks if mask % 2 == 0]
     own_rows = pl.ds(pl.multiple_of(me * rows, 128), rows)
 
     def remote(src, dst, send, recv, **device):
@@ -88,46 +96,98 @@
         slot = lax.rem(e, depth)
         pltpu.make_async_copy(gate_ref.at[0], ring.at[slot], load_sem.at[slot]).wait()
         w = ring[slot]
-        sums[e] = jnp.sum(w * w, axis=0, keepdims=True)
-
-    def send_sums(b):
+        return jnp.sum(w * w, axis=0, keepdims=True)
+
+    def where_of(e):
+        i = lax.rem(e, parts)
+        return lax.div(e, parts), lax.rem(i, 2), lax.div(i, 2)
+
+    def first_square(e, carry):
+        first_in[me, e] = square(e)
+        load(e + LOADS)
+        return carry
+
+    def later_square(e, carry):
+        sums[where_of(e)] = square(e)
+        return carry
+
+    groups = ((0, FIRST), (FIRST, parts - FIRST))
+
+    def send_first(group):
+        part = first_in.at[me, pl.ds(*groups[group])]
         for peer in peers:
-            remote(
-                sums.at[b * parts + peer],
-                sums_in.at[b, me],
-                sum_send.at[b],
-                sum_recv.at[b],
-                zero=peer,
-            ).start()
-
-    def others(ref):
-        return ref.at[pl.ds(0, parts - 1)]
-
-    def finish_sums(b):
-        remote(
-            others(sums_in.at[b]), others(sums_in.at[b]), sum_send.at[b], sum_recv.at[b], zero=me
-        ).wait_recv()
-        sums_in[b, me] = sums[b * parts + me]
-        whole = sums_in[b, 0]
-        for part in range(1, parts):
-            whole = whole + sums_in[b, part]
-        scales[b * parts + me] = jnp.sqrt(whole)
-        row = scales.at[b * parts + me]
-        for peer in peers:
-            remote(row, row, scale_send.at[b], scale_recv.at[b], zero=peer).start()
-
-    def wait_scales(b):
-        remote(
-            others(scales), others(scales), scale_send.at[b], scale_recv.at[b], zero=me
-        ).wait_recv()
+            remote(part, part, first_send.at[group], first_recv.at[group], zero=peer).start()
+
+    def all_first(group):
+        part = first_in.at[pl.ds(0, parts - 1), pl.ds(*groups[group])]
+        return remote(part, part, first_send.at[group], first_recv.at[group], zero=me)
+
+    def finish_first(group):
+        all_first(group).wait_recv()
+        for e in range(groups[group][0], sum(groups[group])):
+            whole = first_in[0, e]
+            for part in range(1, parts):
+                whole = whole + first_in[part, e]
+            scales[0, e % 2, e // 2] = jnp.sqrt(whole)
+
+    def pair_sums(b):
+        return remote(
+            sums.at[b, 1 - side],
+            pair_in.at[b],
+            batch_send.at[0, b],
+            batch_recv.at[0, b],
+            zero=partner,
+        )
+
+    def chip_piece(b, peer):
+        return remote(
+            chip_sums.at[b, lax.div(peer, 2)],
+            chip_in.at[b, place],
+            batch_send.at[1, b],
+            batch_recv.at[1, b],
+            zero=peer,
+        )
+
+    def scale_piece(b, peer):
+        row = scales.at[b, side, place]
+        return remote(row, row, batch_send.at[2, b], batch_recv.at[2, b], zero=peer)
+
+    def pair_scales(b):
+        mine = scales.at[b, side]
+        return remote(mine, mine, batch_send.at[3, b], batch_recv.at[3, b], zero=partner)
+
+    def all_pieces(stage, b):
+        part = chip_in.at[b, pl.ds(0, half - 1)]
+        return remote(part, part, batch_send.at[stage, b], batch_recv.at[stage, b], zero=me)
+
+    def stage_chip(b):
+        pair_sums(b).wait_recv()
+        for q in range(half):
+            chip_sums[b, q] = pair_in[b, q] + sums[b, side, q]
+        chip_in[b, place] = chip_sums[b, place]
+        for peer in cohort:
+            chip_piece(b, peer).start()
+
+    def stage_scale(b):
+        all_pieces(1, b).wait_recv()
+        whole = chip_in[b, 0]
+        for q in range(1, half):
+            whole = whole + chip_in[b, q]
+        scales[b, side, place] = jnp.sqrt(whole)
+        for peer in cohort:
+            scale_piece(b, peer).start()
+
+    def stage_share(b):
+        all_pieces(2, b).wait_recv()
+        pair_scales(b).start()
 
     def keep_scales(b):
-        first = pl.multiple_of(b * parts, 8)
-        whole = jnp.concatenate([scales[b * parts + j] for j in range(parts)], axis=0)
+        start = pl.multiple_of(b * parts, 8)
+        whole = jnp.concatenate([scales[b, j % 2, j // 2] for j in range(parts)], axis=0)
         own = jnp.zeros((parts, width), jnp.float32)
         for part in range(parts):
             own = jnp.where(me == part, whole[:, part * width : (part + 1) * width], own)
-        scale_out[pl.ds(first, parts), :] = own
+        scale_out[pl.ds(start, parts), :] = own
 
     def send_piece(e, slot, at):
         return remote(
@@ -157,7 +217,8 @@
         part = routers.at[pl.ds(0, banks - 1)]
         return remote(part, part, bank_send, bank_recv, zero=me)
 
-    lax.fori_loop(0, depth, lambda e, c: (load(e), c)[1], 0)
+    for e in range(LOADS):
+        load(jnp.int32(e))
 
     barrier = pltpu.get_barrier_semaphore()
     for peer in peers:
@@ -170,66 +231,85 @@
             device_id_type=MESH,
         )
 
-    lax.fori_loop(0, parts, lambda e, c: (square(e), c)[1], 0)
-    pl.semaphore_wait(barrier, parts - 1 + banks - 1)
-    send_sums(0)
     part_router = (router_ref[...] * gain_ref[...]).astype(jnp.bfloat16)
     row_router[...] = part_router
     routers[bank, :, own_rows] = part_router
-    lax.fori_loop(parts, AHEAD * parts, lambda e, c: (square(e), c)[1], 0)
-    finish_sums(0)
-    for b in range(1, AHEAD):
-        send_sums(b)
+    lax.fori_loop(0, FIRST, first_square, 0)
+    pl.semaphore_wait(barrier, parts - 1 + banks - 1)
+    send_first(0)
+    for peer in peers:
+        row_piece(peer).start()
+    lax.fori_loop(FIRST, parts, first_square, 0)
+    send_first(1)
+    finish_first(0)
 
     def step(s, carry):
         b, i = lax.div(s, parts), lax.rem(s, parts)
         slot = lax.rem(s, SLOTS)
 
-        @pl.when(i == 0)
-        def _():
-            wait_scales(b)
+        @pl.when(jnp.logical_and(i == 0, b > 0))
+        def _():
+            pair_scales(b).wait_recv()
 
         @pl.when(s >= SLOTS)
         def _():
             for at in range(parts - 1):
                 send_piece(s, slot, at).wait_send()
 
-        turned = (ring[lax.rem(s, depth)] / scales[s]).T
+        turned = (ring[lax.rem(s, depth)] / scales[where_of(s)]).T
         for part in range(parts):
             outgoing[slot, part] = turned[part * width : (part + 1) * width].astype(
                 jnp.bfloat16
             )
         landing[s, :, own_rows] = outgoing[slot, me]
 
-        @pl.when(s + depth < total)
-        def _():
-            load(s + depth)
+        @pl.when(s + 2 * parts + LOADS < total)
+        def _():
+            load(s + 2 * parts + LOADS)
 
         for at in range(parts - 1):
             send_piece(s, slot, at).start()
 
-        @pl.when(s + AHEAD * parts < total)
-        def _():
-            square(s + AHEAD * parts)
-
-        @pl.when(jnp.logical_and(i == parts - 1, b + AHEAD < batches))
-        def _():
-            send_sums(b + AHEAD)
-
-        @pl.when(jnp.logical_and(i == parts // 2, b + 1 < batches))
-        def _():
-            finish_sums(b + 1)
+        @pl.when(s == 0)
+        def _():
+            def ahead(e, carry):
+                load(e + LOADS)
+                return later_square(e, carry)
+
+            lax.fori_loop(parts, 2 * parts, ahead, 0)
+            pair_sums(1).start()
+
+        @pl.when(s == 1)
+        def _():
+            finish_first(1)
+
+        @pl.when(s + 2 * parts < total)
+        def _():
+            later_square(s + 2 * parts, 0)
+
+        @pl.when(jnp.logical_and(i == parts - 1, b + 2 < batches))
+        def _():
+            pair_sums(b + 2).start()
+
+        @pl.when(b + 1 < batches)
+        def _():
+            @pl.when(i == 1)
+            def _():
+                stage_chip(b + 1)
+
+            @pl.when(i == 3)
+            def _():
+                stage_scale(b + 1)
+
+            @pl.when(i == 5)
+            def _():
+                stage_share(b + 1)
 
         @pl.when(i == 2)
         def _():
             keep_scales(b)
 
-        @pl.when(s == 1)
-        def _():
-            for peer in peers:
-                row_piece(peer).start()
-
-        @pl.when(s == total // 4)
+        @pl.when(s == parts)
         def _():
             all_rows().wait_recv()
             for hop in range(1, banks):
@@ -245,9 +325,13 @@
     turned = routers[...].reshape(banks * router_ref.shape[0], parts * rows).T
     router_out[...] = turned
 
-    for b in range(batches):
-        for sems, buffer in ((sum_send, sums_in.at[0]), (scale_send, scales)):
-            remote(others(buffer), others(buffer), sems.at[b], sems.at[b], zero=me).wait_send()
+    for group in range(2):
+        all_first(group).wait_send()
+    for b in range(1, batches):
+        pair_sums(b).wait_send()
+        all_pieces(1, b).wait_send()
+        all_pieces(2, b).wait_send()
+        pair_scales(b).wait_send()
     for s in range(total - SLOTS, total):
         for at in range(parts - 1):
             send_piece(s, s % SLOTS, at).wait_send()
@@ -264,7 +348,9 @@
     held = router_weight.shape[1]
     vmem = pl.BlockSpec(memory_space=pltpu.VMEM)
     hbm = pl.BlockSpec(memory_space=pl.ANY)
-    depth = (AHEAD + 1) * parts
+    depth = 3 * parts
+    half = parts // 2
+    row = (1, columns)
     dma = pltpu.SemaphoreType.DMA
     return pl.pallas_call(
         functools.partial(exchange_kernel, parts, banks),
@@ -278,18 +364,21 @@
         scratch_shapes=[
             pltpu.VMEM((depth, rows, columns), jnp.float32),
             pltpu.VMEM((SLOTS, parts, width, rows), jnp.bfloat16),
-            pltpu.VMEM((total, 1, columns), jnp.float32),
-            pltpu.VMEM((batches, parts, 1, columns), jnp.float32),
-            pltpu.VMEM((total, 1, columns), jnp.float32),
+            pltpu.VMEM((parts, parts) + row, jnp.float32),
+            pltpu.VMEM((batches, 2, half) + row, jnp.float32),
+            pltpu.VMEM((batches, half) + row, jnp.float32),
+            pltpu.VMEM((batches, half) + row, jnp.float32),
+            pltpu.VMEM((batches, half) + row, jnp.float32),
+            pltpu.VMEM((batches, 2, half) + row, jnp.float32),
             pltpu.VMEM((held, rows), jnp.bfloat16),
             pltpu.VMEM((banks, held, parts * rows), jnp.bfloat16),
             dma((depth,)),
             dma((SLOTS, parts - 1)),
             dma((parts,)),
-            dma((batches,)),
-            dma((batches,)),
-            dma((batches,)),
-            dma((batches,)),
+            dma((2,)),
+            dma((2,)),
+            dma((4, batches)),
+            dma((4, batches)),
             dma,
             dma,
             dma,
@@ -399,7 +488,7 @@
         total = 2 * experts
         power = parts & (parts - 1) == 0 and parts % 8 == 0
         whole = rows % 128 == 0 and columns % (16 * parts) == 0 and held % 16 == 0
-        if power and whole and total % parts == 0 and total >= (AHEAD + 1) * parts:
+        if power and whole and total % parts == 0 and total >= 3 * parts:
             return shards_blocked(parts, banks, w_gate, w_up, router_weight, router_gain)
         return shards_plain(w_gate, w_up, router_weight, router_gain)
 

time: 300 us -> 294 us (0.980)
  Pallas kernels: 299 us -> 293 us
    pallas_call x1, Pallas kernels: 290 us -> 285 us  [exchange(): pl.pallas_call(functools.partial(exchange_kernel, parts, banks), in_specs...]
where the time goes in v2:
time: 294 us
  Pallas kernels  293 us (100%)
    pallas_call x1, Pallas kernels, exchange(): pl.pallas_call(functools.partial(exchange_kernel, parts, banks), in_specs...  285 us
    pallas_call x1, Pallas kernels, deliver(): pl.pallas_call(functools.partial(deliver_kernel, pieces), in_specs=[vmem]...  8.67 us

profile of v2, /device:TPU:0, one launch (start us, length us, event | category | flops | bytes accessed | tf_op | source)
XLA Modules:
  0.0 294.1 jit_solution(15218786988335642460)
XLA Ops:
  0.6 284.8 %exchange.1 = (bf16[64,96,2048]{2,1,0:T(8,128)(2,1)S(1)}, f32[64,96]{1,0:T(8,128)S(1)}, bf16[2048,128]{1,0:T(8,128)(2,1)S(1)}) custom-call(f32[32,256,768]{2,1,0:T(8,128)} %gate_ref.1, f32[32,256,768]{2,1,0:T(8,128)} %up_ref.1, f32[32,256]{1,0:T(8,128)} %bitcast.4, f32[1,256]{1,0:T(1,128)} %bitcast.5), custom_call_target="tpu_custom_call" | custom-call | flops 754974720 | bytes 50331648 | tf_op jit(solution)/shard_map/exchange/pallas_call | solution.py:355
  285.4 8.7 %deliver.1 = (bf16[32,96,2048]{2,1,0:T(8,128)(2,1)}, bf16[32,96,2048]{2,1,0:T(8,128)(2,1)}, f32[32,96]{1,0:T(8,128)}, f32[32,96]{1,0:T(8,128)}, bf16[2048,128]{1,0:T(8,128)(2,1)}) custom-call(bf16[64,96,2048]{2,1,0:T(8,128)(2,1)S(1)} %get-tuple-element.13.landing, f32[64,96]{1,0:T(8,128)S(1)} %get-tuple-element.14.scales, ...), custom_call_target="tpu_custom_call" | custom-call | flops 12582912 | bytes 50331648 | tf_op jit(solution)/shard_map/deliver/pallas_call | solution.py:435

commit v3 on v2

--- a/solution.py
+++ b/solution.py
@@ -207,15 +207,39 @@
         part = routers.at[bank, :, pl.ds(0, (parts - 1) * rows)]
         return remote(part, part, row_send, row_recv, zero=me)
 
-    def bank_piece(step):
-        other = lax.rem(bank + step, banks)
-        return remote(
-            routers.at[bank], routers.at[bank], bank_send, bank_recv, bank=other
-        )
-
-    def all_banks():
-        part = routers.at[pl.ds(0, banks - 1)]
-        return remote(part, part, bank_send, bank_recv, zero=me)
+    def line(hop, send):
+        for way, turn in enumerate((1, -1)):
+            source = bank - turn * (hop - 1 if send else hop)
+            target = bank + turn
+            fits = jnp.logical_and(source >= 0, source < banks)
+            if send:
+                fits = fits & jnp.logical_and(target >= 0, target < banks)
+            yield fits, source, target, (way, hop)
+
+    def line_copy(source, target, at):
+        part = routers.at[source]
+        return remote(part, part, bank_send.at[at], bank_recv.at[at], bank=target)
+
+    def line_start(hop):
+        for fits, source, target, at in line(hop, True):
+
+            @pl.when(fits)
+            def _():
+                line_copy(source, target, at).start()
+
+    def line_arrived(hop):
+        for fits, source, target, at in line(hop, False):
+
+            @pl.when(fits)
+            def _():
+                line_copy(source, bank, at).wait_recv()
+
+    def line_left(hop):
+        for fits, source, target, at in line(hop, True):
+
+            @pl.when(fits)
+            def _():
+                line_copy(source, target, at).wait_send()
 
     for e in range(LOADS):
         load(jnp.int32(e))
@@ -223,19 +247,22 @@
     barrier = pltpu.get_barrier_semaphore()
     for peer in peers:
         pl.semaphore_signal(barrier, inc=1, device_id={"zero": peer}, device_id_type=MESH)
-    for step in range(1, banks):
-        pl.semaphore_signal(
-            barrier,
-            inc=1,
-            device_id={"bank": lax.rem(bank + step, banks)},
-            device_id_type=MESH,
-        )
+    around = jnp.int32(0)
+    for other in (bank - 1, bank + 1):
+        fits = jnp.logical_and(other >= 0, other < banks)
+        around = around + jnp.where(fits, 1, 0)
+
+        @pl.when(fits)
+        def _():
+            pl.semaphore_signal(
+                barrier, inc=1, device_id={"bank": other}, device_id_type=MESH
+            )
 
     part_router = (router_ref[...] * gain_ref[...]).astype(jnp.bfloat16)
     row_router[...] = part_router
     routers[bank, :, own_rows] = part_router
     lax.fori_loop(0, FIRST, first_square, 0)
-    pl.semaphore_wait(barrier, parts - 1 + banks - 1)
+    pl.semaphore_wait(barrier, parts - 1 + around)
     send_first(0)
     for peer in peers:
         row_piece(peer).start()
@@ -309,18 +336,23 @@
         def _():
             keep_scales(b)
 
-        @pl.when(s == parts)
-        def _():
-            all_rows().wait_recv()
-            for hop in range(1, banks):
-                bank_piece(hop).start()
+        for hop in range(1, banks):
+
+            @pl.when(s == hop * parts)
+            def _():
+                if hop == 1:
+                    all_rows().wait_recv()
+                else:
+                    line_arrived(hop - 1)
+                line_start(hop)
 
         return carry
 
     lax.fori_loop(0, total, step, 0)
 
-    all_banks().wait_send()
-    all_banks().wait_recv()
+    line_arrived(banks - 1)
+    for hop in range(1, banks):
+        line_left(hop)
     all_rows().wait_send()
     turned = routers[...].reshape(banks * router_ref.shape[0], parts * rows).T
     router_out[...] = turned
@@ -381,8 +413,8 @@
             dma((4, batches)),
             dma,
             dma,
-            dma,
-            dma,
+            dma((2, banks)),
+            dma((2, banks)),
         ],
         cost_estimate=pl.CostEstimate(
             flops=total * rows * columns * 60,
@@ -488,7 +520,7 @@
         total = 2 * experts
         power = parts & (parts - 1) == 0 and parts % 8 == 0
         whole = rows % 128 == 0 and columns % (16 * parts) == 0 and held % 16 == 0
-        if power and whole and total % parts == 0 and total >= 3 * parts:
+        if power and whole and total % parts == 0 and total >= max(3, banks) * parts:
             return shards_blocked(parts, banks, w_gate, w_up, router_weight, router_gain)
         return shards_plain(w_gate, w_up, router_weight, router_gain)
 

time: 294 us -> 292 us (level)
  no operation moved by 1% of the time
where the time goes in v3:
time: 292 us
  Pallas kernels  292 us (100%)
    pallas_call x1, Pallas kernels, exchange(): pl.pallas_call(functools.partial(exchange_kernel, parts, banks), in_specs...  283 us
    pallas_call x1, Pallas kernels, deliver(): pl.pallas_call(functools.partial(deliver_kernel, pieces), in_specs=[vmem]...  8.67 us

profile of v3, /device:TPU:0, one launch (start us, length us, event | category | flops | bytes accessed | tf_op | source)
XLA Modules:
  0.0 292.2 jit_solution(16486268144949020851)
XLA Ops:
  0.6 282.8 %exchange.1 = (bf16[64,96,2048]{2,1,0:T(8,128)(2,1)S(1)}, f32[64,96]{1,0:T(8,128)S(1)}, bf16[2048,128]{1,0:T(8,128)(2,1)S(1)}) custom-call(f32[32,256,768]{2,1,0:T(8,128)} %gate_ref.1, f32[32,256,768]{2,1,0:T(8,128)} %up_ref.1, f32[32,256]{1,0:T(8,128)} %bitcast.4, f32[1,256]{1,0:T(1,128)} %bitcast.5), custom_call_target="tpu_custom_call" | custom-call | flops 754974720 | bytes 50331648 | tf_op jit(solution)/shard_map/exchange/pallas_call | solution.py:387
  283.5 8.7 %deliver.1 = (bf16[32,96,2048]{2,1,0:T(8,128)(2,1)}, bf16[32,96,2048]{2,1,0:T(8,128)(2,1)}, f32[32,96]{1,0:T(8,128)}, f32[32,96]{1,0:T(8,128)}, bf16[2048,128]{1,0:T(8,128)(2,1)}) custom-call(bf16[64,96,2048]{2,1,0:T(8,128)(2,1)S(1)} %get-tuple-element.13.landing, f32[64,96]{1,0:T(8,128)S(1)} %get-tuple-element.14.scales, ...), custom_call_target="tpu_custom_call" | custom-call | flops 12582912 | bytes 50331648 | tf_op jit(solution)/shard_map/deliver/pallas_call | solution.py:467
